TPU v7x, 32 devices: a whole 2x2x4 slice. The times are simulated.
32 devices in a mesh: scen: 8 (over y, x, core), col: 4 (over z).
Axes of the slice: x: 2, y: 2, z: 4, core: 2. Of those that a mesh axis runs over, the one named last changes fastest.
Arguments:
- tech: bfloat16 [32, 2048, 4096], P('scen', None, 'col'), may hold values from -0.046875 to 0.046875
- recourse: bfloat16 [32, 2048, 1024], P('scen', None, 'col'), may hold values from -0.125 to 0.125
- rhs: float32 [32, 32, 2048], P(None, 'scen'), may hold values from -6 to 6
- cost_first: float32 [4096], P('col'), may hold values from -6 to 6
- cost_second: float32 [32, 1024], P('scen', 'col'), may hold values from -6 to 6
- cone_id: int32 [32, 2048], P('scen'), may hold values from 0 to 127, never falling along the last dimension, each value on 1 to 64 neighbouring positions
Outputs:
- first_section: float32 [32, 4096], P(None, 'col')
- second_section: float32 [32, 32, 1024], P(None, 'scen', 'col')
- slack: float32 [32, 32, 2048], P(None, 'scen', 'col')
- dual: float32 [32, 32, 2048], P(None, 'scen', 'col')
Inputs may be any that keep to these rules, and one draw needn't show every extreme that they name: Along the rows of a scenario cone_id never falls; a cone holds 1 to 64 rows.
All inputs are finite; a program needn't handle non-finite values.
Results may differ from a plain program's by a relative error of at most 0.014.
Values may be sent and summed in bfloat16 or wider, within the bound.
A program may use at most 128 MiB of HBM per device.

v0:
```python
import jax
import jax.numpy as jnp
from jax import lax
from jax.sharding import PartitionSpec as P

NCONE = 128
ITERS = 3
CG_STEPS = 3
HIGH = lax.Precision.HIGHEST


def cone_factors(lead, tail):
    norm_tail = jnp.sqrt(tail)
    inside = norm_tail <= lead
    polar = norm_tail <= -lead
    safe = jnp.where(norm_tail > 0.0, norm_tail, 1.0)
    middle = 0.5 * (lead + norm_tail)
    head = jnp.where(inside, lead, jnp.where(polar, 0.0, middle))
    scale = jnp.where(inside, 1.0, jnp.where(polar, 0.0, middle / safe))
    return (head, scale)


def body(tech, recourse, rhs, cost_first, cost_second, cone_id):
    f32 = jnp.float32
    bf16 = jnp.bfloat16
    n_scen = lax.axis_size("scen")
    n_col = lax.axis_size("col")
    batch = rhs.shape[0]
    scen_local = tech.shape[0]
    rows = tech.shape[1]
    first_cols = tech.shape[2]
    tech_flat = tech.reshape(scen_local * rows, first_cols)
    starts = jnp.concatenate(
        [jnp.ones((scen_local, 1), f32), (cone_id[:, 1:] != cone_id[:, :-1]).astype(f32)], axis=1
    )
    labels = lax.broadcasted_iota(jnp.int32, (1, 1, NCONE), 2)
    onehot = (cone_id[:, :, None] == labels).astype(f32)
    part_rows = rows // n_col
    row_start = lax.axis_index("col") * part_rows
    row_weight = 1.0 / n_col
    share_cols = first_cols // n_scen
    cost_here = lax.dynamic_slice_in_dim(
        cost_first, lax.axis_index("scen") * share_cols, share_cols, 0
    )
    first_weight = 1.0
    start_rows = starts[None]

    def couple(partial_value):
        return lax.psum_scatter(partial_value, "scen", scatter_dimension=1, tiled=True)

    def adjoint(rows_bf):
        first_part = jnp.dot(
            rows_bf.reshape(batch, scen_local * rows), tech_flat, preferred_element_type=f32
        )
        second_part = jnp.einsum("bsm,smk->bsk", rows_bf, recourse, preferred_element_type=f32)
        return (first_part, second_part)

    def local_squares(first_vec, second_vec):
        return first_weight * jnp.sum(first_vec * first_vec, axis=1) + jnp.sum(
            second_vec * second_vec, axis=(1, 2)
        )

    def total_norm(first_vec, second_vec):
        return lax.psum(local_squares(first_vec, second_vec), ("scen", "col"))

    here_rows = rhs.shape[2]
    first_sol = jnp.zeros((batch, share_cols), f32)
    second_sol = jnp.zeros((batch, scen_local, recourse.shape[2]), f32)
    slack = jnp.zeros((batch, scen_local, here_rows), f32)
    dual = jnp.zeros((batch, scen_local, here_rows), f32)
    image = jnp.zeros((batch, scen_local, here_rows), f32)
    for outer in range(ITERS):
        resid_rows = (rhs - slack - dual - image).astype(bf16)
        back_first, back_second = adjoint(resid_rows)
        res_first = couple(back_first) - cost_here[None, :]
        res_second = back_second - cost_second[None]
        res_norm = total_norm(res_first, res_second)
        dir_first, dir_second = (res_first, res_second)
        for step in range(CG_STEPS):
            dir_first_bf = lax.all_gather(dir_first.astype(bf16), "scen", axis=1, tiled=True)
            forward_partial_value = lax.dot_general(
                dir_first_bf, tech_flat, (((1,), (1,)), ((), ())), preferred_element_type=f32
            )
            forward_partial_value = forward_partial_value.reshape(batch, scen_local, rows)
            image_step = lax.psum(
                forward_partial_value
                + jnp.einsum(
                    "bsk,smk->bsm", dir_second.astype(bf16), recourse, preferred_element_type=f32
                ),
                "col",
            )
            curv_term = local_squares(dir_first, dir_second) + row_weight * jnp.sum(
                image_step * image_step, axis=(1, 2)
            )
            curv = lax.psum(curv_term, ("scen", "col"))
            alpha = res_norm / curv
            first_sol = first_sol + alpha[:, None] * dir_first
            second_sol = second_sol + alpha[:, None, None] * dir_second
            image = image + alpha[:, None, None] * image_step
            if step + 1 < CG_STEPS:
                back_first, back_second = adjoint(image_step.astype(bf16))
                res_first = res_first - alpha[:, None] * (dir_first + couple(back_first))
                res_second = res_second - alpha[:, None, None] * (dir_second + back_second)
                new_norm = total_norm(res_first, res_second)
                ratio = new_norm / res_norm
                dir_first = res_first + ratio[:, None] * dir_first
                dir_second = res_second + ratio[:, None, None] * dir_second
                res_norm = new_norm
        values = rhs - image - dual
        project_lead = jnp.einsum("bsm,smc->bsc", values * start_rows, onehot, precision=HIGH)
        project_tail = jnp.einsum(
            "bsm,smc->bsc", values * values * (1.0 - start_rows), onehot, precision=HIGH
        )
        project_lead, project_tail = (project_lead, project_tail)
        head, scale = cone_factors(project_lead, project_tail)
        head_rows = jnp.einsum("bsc,smc->bsm", head, onehot, precision=HIGH)
        scale_rows = jnp.einsum("bsc,smc->bsm", scale, onehot, precision=HIGH)
        slack = start_rows * head_rows + (1.0 - start_rows) * values * scale_rows
        dual = dual + image + slack - rhs
    first_out = lax.all_gather(first_sol, "scen", axis=1, tiled=True)
    slack_out = lax.dynamic_slice_in_dim(slack, row_start, part_rows, 2)
    dual_out = lax.dynamic_slice_in_dim(dual, row_start, part_rows, 2)
    return (first_out, second_sol, slack_out, dual_out)


def solution(mesh):
    placed = (
        P("scen", None, "col"),
        P("scen", None, "col"),
        P(None, "scen", None),
        P("col"),
        P("scen", "col"),
        P("scen", None),
    )
    return jax.shard_map(
        body,
        mesh=mesh,
        in_specs=placed,
        out_specs=(
            P(None, "col"),
            P(None, "scen", "col"),
            P(None, "scen", "col"),
            P(None, "scen", "col"),
        ),
        check_vma=False,
    )
```

profile of v0, /device:TPU:0, one launch (start us, length us, event | category | flops | bytes accessed | tf_op | source)
XLA Modules:
  0.0 1593.4 jit_solution(15257409397023678679)
XLA Ops:
  79.9 52.0 %all-reduce.14.cloned.1.call-done = f32[32,4,2048]{2,0,1:T(8,128)} async-done(((f32[32,4,2048]{2,0,1:T(8,128)}), f32[32,4,2048]{2,0,1:T(8,128)}) %all-reduce.14.cloned.1.call-update) | async-done | bytes 1048592 | tf_op jit(solution)/shard_map/psum | solution.py:85
  142.0 40.0 %all-reduce.3 = (f32[32]{0:T(128)S(1)}, f32[32]{0:T(128)S(1)}) all-reduce(f32[32]{0:T(128)S(1)} %get-tuple-element.49, f32[32]{0:T(128)S(1)} %get-tuple-element.48), channel_id=1, replica_groups=mesh['scen'=8,'col'=4] {'scen','col'}, use_global_device_ids=true, to_apply=%region_3.0 | all-reduce | flops 64 | bytes 512 | tf_op jit(solution)/shard_map/psum | solution.py:64
  186.0 39.4 %psum.192 = f32[32]{0:T(128)S(1)} all-reduce(f32[32]{0:T(128)S(1)} %add.364), channel_id=1, replica_groups=mesh['scen'=8,'col'=4] {'scen','col'}, use_global_device_ids=true, to_apply=%region_10.0 | all-reduce | flops 32 | bytes 256 | tf_op jit(solution)/shard_map/psum | solution.py:64
  251.0 50.4 %all-reduce.16.cloned.1.call-done = f32[32,4,2048]{2,0,1:T(8,128)} async-done(((f32[32,4,2048]{2,0,1:T(8,128)}), f32[32,4,2048]{2,0,1:T(8,128)}) %all-reduce.16.cloned.1.call-update) | async-done | bytes 1048592 | tf_op jit(solution)/shard_map/psum | solution.py:85
  312.7 40.0 %psum.194 = f32[32]{0:T(128)S(1)} all-reduce(f32[32]{0:T(128)S(1)} %multiply_add_fusion.27), channel_id=1, replica_groups=mesh['scen'=8,'col'=4] {'scen','col'}, use_global_device_ids=true, to_apply=%region_15.0 | all-reduce | flops 32 | bytes 256 | tf_op jit(solution)/shard_map/psum | solution.py:95
  356.8 39.2 %psum.195 = f32[32]{0:T(128)S(1)} all-reduce(f32[32]{0:T(128)S(1)} %add.373), channel_id=1, replica_groups=mesh['scen'=8,'col'=4] {'scen','col'}, use_global_device_ids=true, to_apply=%region_19.0 | all-reduce | flops 32 | bytes 256 | tf_op jit(solution)/shard_map/psum | solution.py:64
  422.9 50.0 %all-reduce.18.cloned.1.call-done = f32[32,4,2048]{2,0,1:T(8,128)} async-done(((f32[32,4,2048]{2,0,1:T(8,128)}), f32[32,4,2048]{2,0,1:T(8,128)}) %all-reduce.18.cloned.1.call-update) | async-done | bytes 1048592 | tf_op jit(solution)/shard_map/psum | solution.py:85
  474.5 40.0 %psum.197 = f32[32]{0:T(128)S(1)} all-reduce(f32[32]{0:T(128)S(1)} %multiply_add_fusion.26), channel_id=1, replica_groups=mesh['scen'=8,'col'=4] {'scen','col'}, use_global_device_ids=true, to_apply=%region_24.0 | all-reduce | flops 32 | bytes 256 | tf_op jit(solution)/shard_map/psum | solution.py:95
  597.5 52.0 %all-reduce.20.cloned.1.call-done = f32[32,4,2048]{2,0,1:T(8,128)} async-done(((f32[32,4,2048]{2,0,1:T(8,128)}), f32[32,4,2048]{2,0,1:T(8,128)}) %all-reduce.20.cloned.1.call-update) | async-done | bytes 1048592 | tf_op jit(solution)/shard_map/psum | solution.py:85
  659.7 40.0 %all-reduce.2 = (f32[32]{0:T(128)S(1)}, f32[32]{0:T(128)S(1)}) all-reduce(f32[32]{0:T(128)S(1)} %get-tuple-element.39, f32[32]{0:T(128)S(1)} %get-tuple-element.38), channel_id=1, replica_groups=mesh['scen'=8,'col'=4] {'scen','col'}, use_global_device_ids=true, to_apply=%region_28.29 | all-reduce | flops 64 | bytes 512 | tf_op jit(solution)/shard_map/psum | solution.py:64
  703.7 39.2 %psum.201 = f32[32]{0:T(128)S(1)} all-reduce(f32[32]{0:T(128)S(1)} %add.391), channel_id=1, replica_groups=mesh['scen'=8,'col'=4] {'scen','col'}, use_global_device_ids=true, to_apply=%region_35.36 | all-reduce | flops 32 | bytes 256 | tf_op jit(solution)/shard_map/psum | solution.py:64
  768.7 50.4 %all-reduce.22.cloned.1.call-done = f32[32,4,2048]{2,0,1:T(8,128)} async-done(((f32[32,4,2048]{2,0,1:T(8,128)}), f32[32,4,2048]{2,0,1:T(8,128)}) %all-reduce.22.cloned.1.call-update) | async-done | bytes 1048592 | tf_op jit(solution)/shard_map/psum | solution.py:85
  830.4 40.0 %psum.203 = f32[32]{0:T(128)S(1)} all-reduce(f32[32]{0:T(128)S(1)} %multiply_add_fusion.24), channel_id=1, replica_groups=mesh['scen'=8,'col'=4] {'scen','col'}, use_global_device_ids=true, to_apply=%region_40.41 | all-reduce | flops 32 | bytes 256 | tf_op jit(solution)/shard_map/psum | solution.py:95
  874.5 39.2 %psum.204 = f32[32]{0:T(128)S(1)} all-reduce(f32[32]{0:T(128)S(1)} %add.400), channel_id=1, replica_groups=mesh['scen'=8,'col'=4] {'scen','col'}, use_global_device_ids=true, to_apply=%region_44.45 | all-reduce | flops 32 | bytes 256 | tf_op jit(solution)/shard_map/psum | solution.py:64
  941.0 50.3 %all-reduce.24.cloned.1.call-done = f32[32,4,2048]{2,0,1:T(8,128)} async-done(((f32[32,4,2048]{2,0,1:T(8,128)}), f32[32,4,2048]{2,0,1:T(8,128)}) %all-reduce.24.cloned.1.call-update) | async-done | bytes 1048592 | tf_op jit(solution)/shard_map/psum | solution.py:85
  992.7 40.0 %psum.206 = f32[32]{0:T(128)S(1)} all-reduce(f32[32]{0:T(128)S(1)} %multiply_add_fusion.23), channel_id=1, replica_groups=mesh['scen'=8,'col'=4] {'scen','col'}, use_global_device_ids=true, to_apply=%region_49.50 | all-reduce | flops 32 | bytes 256 | tf_op jit(solution)/shard_map/psum | solution.py:95
  1117.1 52.0 %all-reduce.26.cloned.1.call-done = f32[32,4,2048]{2,0,1:T(8,128)} async-done(((f32[32,4,2048]{2,0,1:T(8,128)}), f32[32,4,2048]{2,0,1:T(8,128)}) %all-reduce.26.cloned.1.call-update) | async-done | bytes 1048592 | tf_op jit(solution)/shard_map/psum | solution.py:85
  1179.3 40.0 %all-reduce.1 = (f32[32]{0:T(128)S(1)}, f32[32]{0:T(128)S(1)}) all-reduce(f32[32]{0:T(128)S(1)} %get-tuple-element.25, f32[32]{0:T(128)S(1)} %get-tuple-element.24), channel_id=1, replica_groups=mesh['scen'=8,'col'=4] {'scen','col'}, use_global_device_ids=true, to_apply=%region_53.54 | all-reduce | flops 64 | bytes 512 | tf_op jit(solution)/shard_map/psum | solution.py:64
  1223.3 39.2 %psum.210 = f32[32]{0:T(128)S(1)} all-reduce(f32[32]{0:T(128)S(1)} %add.420), channel_id=1, replica_groups=mesh['scen'=8,'col'=4] {'scen','col'}, use_global_device_ids=true, to_apply=%region_60.61 | all-reduce | flops 32 | bytes 256 | tf_op jit(solution)/shard_map/psum | solution.py:64
  1288.4 50.4 %all-reduce.28.cloned.1.call-done = f32[32,4,2048]{2,0,1:T(8,128)} async-done(((f32[32,4,2048]{2,0,1:T(8,128)}), f32[32,4,2048]{2,0,1:T(8,128)}) %all-reduce.28.cloned.1.call-update) | async-done | bytes 1048592 | tf_op jit(solution)/shard_map/psum | solution.py:85
  1350.1 40.0 %psum.212 = f32[32]{0:T(128)S(1)} all-reduce(f32[32]{0:T(128)S(1)} %multiply_add_fusion.21), channel_id=1, replica_groups=mesh['scen'=8,'col'=4] {'scen','col'}, use_global_device_ids=true, to_apply=%region_65.66 | all-reduce | flops 32 | bytes 256 | tf_op jit(solution)/shard_map/psum | solution.py:95
  1394.2 39.2 %psum.213 = f32[32]{0:T(128)S(1)} all-reduce(f32[32]{0:T(128)S(1)} %add.429), channel_id=1, replica_groups=mesh['scen'=8,'col'=4] {'scen','col'}, use_global_device_ids=true, to_apply=%region_69.70 | all-reduce | flops 32 | bytes 256 | tf_op jit(solution)/shard_map/psum | solution.py:64
  1462.7 48.7 %all-reduce.30.cloned.1.call-done = f32[32,4,2048]{2,0,1:T(8,128)} async-done(((f32[32,4,2048]{2,0,1:T(8,128)}), f32[32,4,2048]{2,0,1:T(8,128)}) %all-reduce.30.cloned.1.call-update) | async-done | bytes 1048592 | tf_op jit(solution)/shard_map/psum | solution.py:85
  1514.0 40.1 %psum.215 = f32[32]{0:T(128)} all-reduce(f32[32]{0:T(128)} %multiply_add_fusion.20), channel_id=1, replica_groups=mesh['scen'=8,'col'=4] {'scen','col'}, use_global_device_ids=true, to_apply=%region_74.75 | all-reduce | flops 32 | bytes 256 | tf_op jit(solution)/shard_map/psum | solution.py:95
  (300 shorter events, 526.6 us)
Async XLA Ops:
  7.2 47.4 %reduce-scatter.10.cloned.1.call-start = ((), (), s32[]{:S(2)}) async-start(), calls=%async_computation.9 | async-start | bytes 147456 | tf_op jit(solution)/shard_map/reduce_scatter | solution.py:49
  18.1 113.7 %all-reduce.14.cloned.1.call-start = ((), (), s32[]{:S(2)}) async-start(), calls=%async_computation.10 | async-start | bytes 2097152 | tf_op jit(solution)/shard_map/psum | solution.py:85
  18.9 1243.5 %copy-start.43 = (f32[128]{0:T(128)}, f32[128]{0:T(128)S(1)}, u32[]{:S(2)}) copy-start(f32[128]{0:T(128)S(1)} %dynamic_slice.9) | copy-start | bytes 1540
  22.1 225.1 %copy-start.24 = (f32[32,4,256]{2,0,1:T(8,128)}, f32[32,4,256]{2,0,1:T(8,128)S(1)}, u32[]{:S(2)}) copy-start(f32[32,4,256]{2,0,1:T(8,128)S(1)} %get-tuple-element.60) | copy-start | bytes 393220
  79.8 105.3 %reduce-scatter.12.cloned.1.call-start = ((), (), s32[]{:S(2)}) async-start(), calls=%async_computation.11 | async-start | bytes 147456 | tf_op jit(solution)/shard_map/reduce_scatter | solution.py:49
  141.7 159.7 %all-reduce.16.cloned.1.call-start = ((), (), s32[]{:S(2)}) async-start(), calls=%async_computation.12 | async-start | bytes 2097152 | tf_op jit(solution)/shard_map/psum | solution.py:85
  181.9 332.5 %copy-start.49 = (f32[32]{0:T(128)}, f32[32]{0:T(128)S(1)}, u32[]{:S(2)}) copy-start(f32[32]{0:T(128)S(1)} %div.54) | copy-start | bytes 388
  251.0 104.9 %reduce-scatter.14.cloned.1.call-start = ((), (), s32[]{:S(2)}) async-start(), calls=%async_computation.13 | async-start | bytes 147456 | tf_op jit(solution)/shard_map/reduce_scatter | solution.py:49
  312.7 160.3 %all-reduce.18.cloned.1.call-start = ((), (), s32[]{:S(2)}) async-start(), calls=%async_computation.14 | async-start | bytes 2097152 | tf_op jit(solution)/shard_map/psum | solution.py:85
  422.5 149.7 %reduce-scatter.16.cloned.1.call-start = ((), (), s32[]{:S(2)}) async-start(), calls=%async_computation.15 | async-start | bytes 147456 | tf_op jit(solution)/shard_map/reduce_scatter | solution.py:49
  422.7 618.7 %copy-start.44 = (f32[4,2048]{1,0:T(4,128)}, f32[4,2048]{1,0:T(4,128)S(1)}, u32[]{:S(2)}) copy-start(f32[4,2048]{1,0:T(4,128)S(1)} %broadcast_subtract_fusion) | copy-start | bytes 98308
  474.5 570.3 %copy-start.35 = (f32[4,2048]{1,0:T(4,128)}, f32[4,2048]{1,0:T(4,128)S(1)}, u32[]{:S(2)}) copy-start(f32[4,2048]{1,0:T(4,128)S(1)} %pad_convert_fusion) | copy-start | bytes 98308
  539.1 110.4 %all-reduce.20.cloned.1.call-start = ((), (), s32[]{:S(2)}) async-start(), calls=%async_computation.16 | async-start | bytes 2097152 | tf_op jit(solution)/shard_map/psum | solution.py:85
  597.5 105.3 %reduce-scatter.18.cloned.1.call-start = ((), (), s32[]{:S(2)}) async-start(), calls=%async_computation.17 | async-start | bytes 147456 | tf_op jit(solution)/shard_map/reduce_scatter | solution.py:49
  659.4 159.7 %all-reduce.22.cloned.1.call-start = ((), (), s32[]{:S(2)}) async-start(), calls=%async_computation.18 | async-start | bytes 2097152 | tf_op jit(solution)/shard_map/psum | solution.py:85
  699.6 333.1 %copy-start.50 = (f32[32]{0:T(128)}, f32[32]{0:T(128)S(1)}, u32[]{:S(2)}) copy-start(f32[32]{0:T(128)S(1)} %div.60) | copy-start | bytes 388
  768.6 104.9 %reduce-scatter.20.cloned.1.call-start = ((), (), s32[]{:S(2)}) async-start(), calls=%async_computation.19 | async-start | bytes 147456 | tf_op jit(solution)/shard_map/reduce_scatter | solution.py:49
  830.4 160.9 %all-reduce.24.cloned.1.call-start = ((), (), s32[]{:S(2)}) async-start(), calls=%async_computation.20 | async-start | bytes 2097152 | tf_op jit(solution)/shard_map/psum | solution.py:85
  940.8 151.0 %reduce-scatter.22.cloned.1.call-start = ((), (), s32[]{:S(2)}) async-start(), calls=%async_computation.21 | async-start | bytes 147456 | tf_op jit(solution)/shard_map/reduce_scatter | solution.py:49
  1058.7 110.4 %all-reduce.26.cloned.1.call-start = ((), (), s32[]{:S(2)}) async-start(), calls=%async_computation.22 | async-start | bytes 2097152 | tf_op jit(solution)/shard_map/psum | solution.py:85
  1117.1 105.3 %reduce-scatter.24.cloned.1.call-start = ((), (), s32[]{:S(2)}) async-start(), calls=%async_computation.23 | async-start | bytes 147456 | tf_op jit(solution)/shard_map/reduce_scatter | solution.py:49
  1179.0 159.8 %all-reduce.28.cloned.1.call-start = ((), (), s32[]{:S(2)}) async-start(), calls=%async_computation.24 | async-start | bytes 2097152 | tf_op jit(solution)/shard_map/psum | solution.py:85
  1288.3 104.9 %reduce-scatter.26.cloned.1.call-start = ((), (), s32[]{:S(2)}) async-start(), calls=%async_computation.25 | async-start | bytes 147456 | tf_op jit(solution)/shard_map/reduce_scatter | solution.py:49
  1350.1 161.3 %all-reduce.30.cloned.1.call-start = ((), (), s32[]{:S(2)}) async-start(), calls=%async_computation.26 | async-start | bytes 2097152 | tf_op jit(solution)/shard_map/psum | solution.py:85
  (52 other events, 2448.2 us)
Sparse Core Ops, SparseCore 0:
  18.2 36.2 reduce-scatter.9
  79.9 51.8 all-reduce.13
  141.8 32.8 reduce-scatter.11
  251.1 50.3 all-reduce.15
  312.8 32.8 reduce-scatter.13
  422.6 50.3 all-reduce.17
  539.2 32.8 reduce-scatter.15
  597.6 51.8 all-reduce.19
  659.5 32.8 reduce-scatter.17
  768.7 50.3 all-reduce.21
  830.5 32.8 reduce-scatter.19
  940.9 50.3 all-reduce.23
  1058.9 32.8 reduce-scatter.21
  1117.2 51.8 all-reduce.25
  1179.1 32.8 reduce-scatter.23
  1288.4 50.3 all-reduce.27
  1350.2 32.8 reduce-scatter.25
  1461.0 50.3 all-reduce.29
where the time goes:
time: 1610 us; the launch traced here: 1590 us
  blocking collectives  692 us (43%)
  waiting for transfers between devices  549 us (34%)
  matrix products  292 us (18%)
  other arithmetic  39.5 us (2%)
    psum x9, waiting for transfers between devices, body(): lax.psum(forward_partial_value + jnp.einsum('bsk,smk->bsm', dir_second.as...  456 us
    psum x9, blocking collectives, total_norm(): return lax.psum(local_squares(first_vec, second_vec), ('scen', 'col'))  355 us
    psum x6, blocking collectives, body(): curv = lax.psum(curv_term, ('scen', 'col'))  240 us
    dot_general x9, matrix products, body(): lax.dot_general(dir_first_bf, tech_flat, (((1,), (1,)), ((), ())), prefer...  107 us
    reduce_scatter x9, waiting for transfers between devices, couple(): lax.psum_scatter(partial_value, 'scen', scatter_dimension=1, tiled=True)  92.3 us
    dot_general x9, matrix products, adjoint(): jnp.dot(rows_bf.reshape(batch, scen_local * rows), tech_flat, preferred_e...  87.1 us
    all_gather x9, blocking collectives, body(): lax.all_gather(dir_first.astype(bf16), 'scen', axis=1, tiled=True)  86.4 us
  transfers between devices with their start and end apart: 18, of which 12 were waited for; matrix products, arithmetic and copies ran while one was open for 2% of the time, Pallas kernels for 0%

commit v1 on v0

--- a/solution.py
+++ b/solution.py
@@ -7,6 +7,7 @@
 ITERS = 3
 CG_STEPS = 3
 HIGH = lax.Precision.HIGHEST
+sections_turn = lambda base_x: lax.psum(lax.psum(base_x, "col"), "scen")
 
 
 def cone_factors(lead, tail):
@@ -61,7 +62,7 @@
         )
 
     def total_norm(first_vec, second_vec):
-        return lax.psum(local_squares(first_vec, second_vec), ("scen", "col"))
+        return sections_turn(local_squares(first_vec, second_vec))
 
     here_rows = rhs.shape[2]
     first_sol = jnp.zeros((batch, share_cols), f32)

time: 1610 us -> 1550 us (0.963)
  blocking collectives: 692 us -> 648 us
    psum x9 -> x18, blocking collectives: 355 us -> 198 us  [sections_turn = lambda base_x: lax.psum(lax.psum(base_x, 'col'), 'scen')]
    psum x6 -> x9, blocking collectives: 240 us -> 354 us  [body(): curv = lax.psum(curv_term, ('scen', 'col'))]
where the time goes in v1:
time: 1550 us; the launch traced here: 1540 us
  blocking collectives  648 us (42%)
  waiting for transfers between devices  542 us (35%)
  matrix products  292 us (19%)
  other arithmetic  39.5 us (3%)
  between operations  15.6 us (1%)
    psum x9, waiting for transfers between devices, body(): lax.psum(forward_partial_value + jnp.einsum('bsk,smk->bsm', dir_second.as...  449 us
    psum x9, blocking collectives, body(): curv = lax.psum(curv_term, ('scen', 'col'))  354 us
    psum x18, blocking collectives, sections_turn = lambda base_x: lax.psum(lax.psum(base_x, 'col'), 'scen')  198 us
    dot_general x9, matrix products, body(): lax.dot_general(dir_first_bf, tech_flat, (((1,), (1,)), ((), ())), prefer...  107 us
    reduce_scatter x9, waiting for transfers between devices, couple(): lax.psum_scatter(partial_value, 'scen', scatter_dimension=1, tiled=True)  92.3 us
    dot_general x9, matrix products, adjoint(): jnp.dot(rows_bf.reshape(batch, scen_local * rows), tech_flat, preferred_e...  87.1 us
    all_gather x9, blocking collectives, body(): lax.all_gather(dir_first.astype(bf16), 'scen', axis=1, tiled=True)  86.1 us
    dot_general x9, matrix products, body(): jnp.einsum('bsk,smk->bsm', dir_second.astype(bf16), recourse, preferred_e...  32.1 us
  transfers between devices with their start and end apart: 18, of which 12 were waited for; matrix products, arithmetic and copies ran while one was open for 2% of the time, Pallas kernels for 0%

profile of v1, /device:TPU:0, one launch (start us, length us, event | category | flops | bytes accessed | tf_op | source)
XLA Modules:
  0.0 1542.6 jit_solution(11445897033024370043)
XLA Ops:
  22.1 32.4 %reduce-scatter.10.cloned.1.call-done = f32[32,128]{1,0:T(8,128)} async-done(((f32[32,1024]{1,0:T(8,128)}), f32[32,128]{1,0:T(8,128)}) %reduce-scatter.10.cloned.1.call-update) | async-done | bytes 16400 | tf_op jit(solution)/shard_map/reduce_scatter | solution.py:50
  64.2 12.0 fusion.136
  79.9 52.0 %all-reduce.11.cloned.1.call-done = f32[32,4,2048]{2,0,1:T(8,128)} async-done(((f32[32,4,2048]{2,0,1:T(8,128)}), f32[32,4,2048]{2,0,1:T(8,128)}) %all-reduce.11.cloned.1.call-update) | async-done | bytes 1048592 | tf_op jit(solution)/shard_map/psum | solution.py:86
  163.8 38.2 %psum.255 = f32[32]{0:T(128)S(1)} all-reduce(f32[32]{0:T(128)S(1)} %get-tuple-element.42), channel_id=1, replica_groups=mesh['scen'=8,'col'=4] {'scen','col'}, use_global_device_ids=true, to_apply=%region_7.0 | all-reduce | flops 32 | bytes 256 | tf_op jit(solution)/shard_map/psum | solution.py:96
  216.2 12.0 psum.257
  253.6 49.2 %all-reduce.13.cloned.1.call-done = f32[32,4,2048]{2,0,1:T(8,128)} async-done(((f32[32,4,2048]{2,0,1:T(8,128)}), f32[32,4,2048]{2,0,1:T(8,128)}) %all-reduce.13.cloned.1.call-update) | async-done | bytes 1048592 | tf_op jit(solution)/shard_map/psum | solution.py:86
  314.1 40.0 %psum.259 = f32[32]{0:T(128)S(1)} all-reduce(f32[32]{0:T(128)S(1)} %multiply_add_fusion.27), channel_id=1, replica_groups=mesh['scen'=8,'col'=4] {'scen','col'}, use_global_device_ids=true, to_apply=%region_17.0 | all-reduce | flops 32 | bytes 256 | tf_op jit(solution)/shard_map/psum | solution.py:96
  407.2 48.9 %all-reduce.15.cloned.1.call-done = f32[32,4,2048]{2,0,1:T(8,128)} async-done(((f32[32,4,2048]{2,0,1:T(8,128)}), f32[32,4,2048]{2,0,1:T(8,128)}) %all-reduce.15.cloned.1.call-update) | async-done | bytes 1048592 | tf_op jit(solution)/shard_map/psum | solution.py:86
  457.6 40.0 %psum.263 = f32[32]{0:T(128)S(1)} all-reduce(f32[32]{0:T(128)S(1)} %multiply_add_fusion.26), channel_id=1, replica_groups=mesh['scen'=8,'col'=4] {'scen','col'}, use_global_device_ids=true, to_apply=%region_27.0 | all-reduce | flops 32 | bytes 256 | tf_op jit(solution)/shard_map/psum | solution.py:96
  525.4 29.9 %reduce-scatter.16.cloned.1.call-done = f32[32,128]{1,0:T(8,128)} async-done(((f32[32,1024]{1,0:T(8,128)}), f32[32,128]{1,0:T(8,128)}) %reduce-scatter.16.cloned.1.call-update) | async-done | bytes 16400 | tf_op jit(solution)/shard_map/reduce_scatter | solution.py:50
  580.6 52.0 %all-reduce.17.cloned.1.call-done = f32[32,4,2048]{2,0,1:T(8,128)} async-done(((f32[32,4,2048]{2,0,1:T(8,128)}), f32[32,4,2048]{2,0,1:T(8,128)}) %all-reduce.17.cloned.1.call-update) | async-done | bytes 1048592 | tf_op jit(solution)/shard_map/psum | solution.py:86
  664.6 38.0 %psum.267 = f32[32]{0:T(128)S(1)} all-reduce(f32[32]{0:T(128)S(1)} %get-tuple-element.32), channel_id=1, replica_groups=mesh['scen'=8,'col'=4] {'scen','col'}, use_global_device_ids=true, to_apply=%region_35.36 | all-reduce | flops 32 | bytes 256 | tf_op jit(solution)/shard_map/psum | solution.py:96
  754.4 49.2 %all-reduce.19.cloned.1.call-done = f32[32,4,2048]{2,0,1:T(8,128)} async-done(((f32[32,4,2048]{2,0,1:T(8,128)}), f32[32,4,2048]{2,0,1:T(8,128)}) %all-reduce.19.cloned.1.call-update) | async-done | bytes 1048592 | tf_op jit(solution)/shard_map/psum | solution.py:86
  814.9 40.0 %psum.271 = f32[32]{0:T(128)S(1)} all-reduce(f32[32]{0:T(128)S(1)} %multiply_add_fusion.24), channel_id=1, replica_groups=mesh['scen'=8,'col'=4] {'scen','col'}, use_global_device_ids=true, to_apply=%region_45.46 | all-reduce | flops 32 | bytes 256 | tf_op jit(solution)/shard_map/psum | solution.py:96
  908.4 49.1 %all-reduce.21.cloned.1.call-done = f32[32,4,2048]{2,0,1:T(8,128)} async-done(((f32[32,4,2048]{2,0,1:T(8,128)}), f32[32,4,2048]{2,0,1:T(8,128)}) %all-reduce.21.cloned.1.call-update) | async-done | bytes 1048592 | tf_op jit(solution)/shard_map/psum | solution.py:86
  958.9 40.0 %psum.275 = f32[32]{0:T(128)S(1)} all-reduce(f32[32]{0:T(128)S(1)} %multiply_add_fusion.23), channel_id=1, replica_groups=mesh['scen'=8,'col'=4] {'scen','col'}, use_global_device_ids=true, to_apply=%region_55.56 | all-reduce | flops 32 | bytes 256 | tf_op jit(solution)/shard_map/psum | solution.py:96
  1028.1 29.9 %reduce-scatter.22.cloned.1.call-done = f32[32,128]{1,0:T(8,128)} async-done(((f32[32,1024]{1,0:T(8,128)}), f32[32,128]{1,0:T(8,128)}) %reduce-scatter.22.cloned.1.call-update) | async-done | bytes 16400 | tf_op jit(solution)/shard_map/reduce_scatter | solution.py:50
  1083.3 52.0 %all-reduce.23.cloned.1.call-done = f32[32,4,2048]{2,0,1:T(8,128)} async-done(((f32[32,4,2048]{2,0,1:T(8,128)}), f32[32,4,2048]{2,0,1:T(8,128)}) %all-reduce.23.cloned.1.call-update) | async-done | bytes 1048592 | tf_op jit(solution)/shard_map/psum | solution.py:86
  1167.3 38.0 %psum.279 = f32[32]{0:T(128)S(1)} all-reduce(f32[32]{0:T(128)S(1)} %get-tuple-element.18), channel_id=1, replica_groups=mesh['scen'=8,'col'=4] {'scen','col'}, use_global_device_ids=true, to_apply=%region_63.64 | all-reduce | flops 32 | bytes 256 | tf_op jit(solution)/shard_map/psum | solution.py:96
  1219.4 11.9 psum.281
  1257.1 49.2 %all-reduce.25.cloned.1.call-done = f32[32,4,2048]{2,0,1:T(8,128)} async-done(((f32[32,4,2048]{2,0,1:T(8,128)}), f32[32,4,2048]{2,0,1:T(8,128)}) %all-reduce.25.cloned.1.call-update) | async-done | bytes 1048592 | tf_op jit(solution)/shard_map/psum | solution.py:86
  1317.7 40.0 %psum.283 = f32[32]{0:T(128)S(1)} all-reduce(f32[32]{0:T(128)S(1)} %multiply_add_fusion.21), channel_id=1, replica_groups=mesh['scen'=8,'col'=4] {'scen','col'}, use_global_device_ids=true, to_apply=%region_73.74 | all-reduce | flops 32 | bytes 256 | tf_op jit(solution)/shard_map/psum | solution.py:96
  1413.1 47.5 %all-reduce.27.cloned.1.call-done = f32[32,4,2048]{2,0,1:T(8,128)} async-done(((f32[32,4,2048]{2,0,1:T(8,128)}), f32[32,4,2048]{2,0,1:T(8,128)}) %all-reduce.27.cloned.1.call-update) | async-done | bytes 1048592 | tf_op jit(solution)/shard_map/psum | solution.py:86
  1463.2 40.1 %psum.287 = f32[32]{0:T(128)} all-reduce(f32[32]{0:T(128)} %multiply_add_fusion.20), channel_id=1, replica_groups=mesh['scen'=8,'col'=4] {'scen','col'}, use_global_device_ids=true, to_apply=%region_83.84 | all-reduce | flops 32 | bytes 256 | tf_op jit(solution)/shard_map/psum | solution.py:96
  (312 shorter events, 595.9 us)
Async XLA Ops:
  7.2 47.4 %reduce-scatter.10.cloned.1.call-start = ((), (), s32[]{:S(2)}) async-start(), calls=%async_computation.9 | async-start | bytes 147456 | tf_op jit(solution)/shard_map/reduce_scatter | solution.py:50
  18.1 113.7 %all-reduce.11.cloned.1.call-start = ((), (), s32[]{:S(2)}) async-start(), calls=%async_computation.10 | async-start | bytes 2097152 | tf_op jit(solution)/shard_map/psum | solution.py:86
  18.9 1212.4 %copy-start.43 = (f32[128]{0:T(128)}, f32[128]{0:T(128)S(1)}, u32[]{:S(2)}) copy-start(f32[128]{0:T(128)S(1)} %dynamic_slice.9) | copy-start | bytes 1540
  22.1 227.7 %copy-start.24 = (f32[32,4,256]{2,0,1:T(8,128)}, f32[32,4,256]{2,0,1:T(8,128)S(1)}, u32[]{:S(2)}) copy-start(f32[32,4,256]{2,0,1:T(8,128)S(1)} %get-tuple-element.54) | copy-start | bytes 393220
  79.8 125.3 %reduce-scatter.12.cloned.1.call-start = ((), (), s32[]{:S(2)}) async-start(), calls=%async_computation.11 | async-start | bytes 147456 | tf_op jit(solution)/shard_map/reduce_scatter | solution.py:50
  141.7 161.1 %all-reduce.13.cloned.1.call-start = ((), (), s32[]{:S(2)}) async-start(), calls=%async_computation.12 | async-start | bytes 2097152 | tf_op jit(solution)/shard_map/psum | solution.py:86
  202.0 295.6 %copy-start.49 = (f32[32]{0:T(128)}, f32[32]{0:T(128)S(1)}, u32[]{:S(2)}) copy-start(f32[32]{0:T(128)S(1)} %div.54) | copy-start | bytes 388
  253.6 103.7 %reduce-scatter.14.cloned.1.call-start = ((), (), s32[]{:S(2)}) async-start(), calls=%async_computation.13 | async-start | bytes 147456 | tf_op jit(solution)/shard_map/reduce_scatter | solution.py:50
  314.1 142.0 %all-reduce.15.cloned.1.call-start = ((), (), s32[]{:S(2)}) async-start(), calls=%async_computation.14 | async-start | bytes 2097152 | tf_op jit(solution)/shard_map/psum | solution.py:86
  406.8 148.5 %reduce-scatter.16.cloned.1.call-start = ((), (), s32[]{:S(2)}) async-start(), calls=%async_computation.15 | async-start | bytes 147456 | tf_op jit(solution)/shard_map/reduce_scatter | solution.py:50
  407.0 600.6 %copy-start.44 = (f32[4,2048]{1,0:T(4,128)}, f32[4,2048]{1,0:T(4,128)S(1)}, u32[]{:S(2)}) copy-start(f32[4,2048]{1,0:T(4,128)S(1)} %broadcast_subtract_fusion) | copy-start | bytes 98308
  457.6 553.4 %copy-start.35 = (f32[4,2048]{1,0:T(4,128)}, f32[4,2048]{1,0:T(4,128)S(1)}, u32[]{:S(2)}) copy-start(f32[4,2048]{1,0:T(4,128)S(1)} %pad_convert_fusion) | copy-start | bytes 98308
  522.2 110.4 %all-reduce.17.cloned.1.call-start = ((), (), s32[]{:S(2)}) async-start(), calls=%async_computation.16 | async-start | bytes 2097152 | tf_op jit(solution)/shard_map/psum | solution.py:86
  580.6 125.1 %reduce-scatter.18.cloned.1.call-start = ((), (), s32[]{:S(2)}) async-start(), calls=%async_computation.17 | async-start | bytes 147456 | tf_op jit(solution)/shard_map/reduce_scatter | solution.py:50
  642.5 161.1 %all-reduce.19.cloned.1.call-start = ((), (), s32[]{:S(2)}) async-start(), calls=%async_computation.18 | async-start | bytes 2097152 | tf_op jit(solution)/shard_map/psum | solution.py:86
  702.6 296.3 %copy-start.50 = (f32[32]{0:T(128)}, f32[32]{0:T(128)S(1)}, u32[]{:S(2)}) copy-start(f32[32]{0:T(128)S(1)} %div.60) | copy-start | bytes 388
  754.3 103.7 %reduce-scatter.20.cloned.1.call-start = ((), (), s32[]{:S(2)}) async-start(), calls=%async_computation.19 | async-start | bytes 147456 | tf_op jit(solution)/shard_map/reduce_scatter | solution.py:50
  814.9 142.6 %all-reduce.21.cloned.1.call-start = ((), (), s32[]{:S(2)}) async-start(), calls=%async_computation.20 | async-start | bytes 2097152 | tf_op jit(solution)/shard_map/psum | solution.py:86
  908.2 149.8 %reduce-scatter.22.cloned.1.call-start = ((), (), s32[]{:S(2)}) async-start(), calls=%async_computation.21 | async-start | bytes 147456 | tf_op jit(solution)/shard_map/reduce_scatter | solution.py:50
  1024.9 110.4 %all-reduce.23.cloned.1.call-start = ((), (), s32[]{:S(2)}) async-start(), calls=%async_computation.22 | async-start | bytes 2097152 | tf_op jit(solution)/shard_map/psum | solution.py:86
  1083.3 125.1 %reduce-scatter.24.cloned.1.call-start = ((), (), s32[]{:S(2)}) async-start(), calls=%async_computation.23 | async-start | bytes 147456 | tf_op jit(solution)/shard_map/reduce_scatter | solution.py:50
  1145.2 161.2 %all-reduce.25.cloned.1.call-start = ((), (), s32[]{:S(2)}) async-start(), calls=%async_computation.24 | async-start | bytes 2097152 | tf_op jit(solution)/shard_map/psum | solution.py:86
  1257.1 103.7 %reduce-scatter.26.cloned.1.call-start = ((), (), s32[]{:S(2)}) async-start(), calls=%async_computation.25 | async-start | bytes 147456 | tf_op jit(solution)/shard_map/reduce_scatter | solution.py:50
  1317.6 143.0 %all-reduce.27.cloned.1.call-start = ((), (), s32[]{:S(2)}) async-start(), calls=%async_computation.26 | async-start | bytes 2097152 | tf_op jit(solution)/shard_map/psum | solution.py:86
  (52 other events, 2349.2 us)
Sparse Core Ops, SparseCore 0:
  18.2 36.2 reduce-scatter.9
  79.9 51.8 all-reduce.10
  141.8 32.8 reduce-scatter.11
  253.7 49.1 all-reduce.12
  314.2 32.8 reduce-scatter.13
  406.9 49.1 all-reduce.14
  522.3 32.8 reduce-scatter.15
  580.7 51.9 all-reduce.16
  642.6 32.8 reduce-scatter.17
  754.5 49.1 all-reduce.18
  815.0 32.8 reduce-scatter.19
  908.3 49.1 all-reduce.20
  1025.0 32.8 reduce-scatter.21
  1083.4 51.8 all-reduce.22
  1145.3 32.8 reduce-scatter.23
  1257.2 49.0 all-reduce.24
  1317.7 32.8 reduce-scatter.25
  1411.5 49.1 all-reduce.26
